TPU v7x, 32 devices: a whole 2x2x4 slice. The times are simulated.
32 devices in a mesh: lang: 2 (over y), clu: 16 (over z, x, core).
Axes of the slice: x: 2, y: 2, z: 4, core: 2. Of those that a mesh axis runs over, the one named last changes fastest.
Arguments:
- embeddings: bfloat16 [8192, 1024], P(('lang', 'clu')), parts along dimension 0, may hold values from -6 to 6
- assignment: int32 [8192, 1], P(('lang', 'clu')), parts along dimension 0, may hold values from 0 to 31; in each aligned block of 256 rows (0 to 255, 256 to 511, ...) at most 16 rows name the same one
Outputs:
- best_similarity: float32 [8192], P(('lang', 'clu')), parts along dimension 0
There are 2 independent parts, one for each index of `lang`. A program takes and returns all parts, laid end to end along the dimension named above; each array names one. Nothing has to cross between parts.
Inputs may be any that keep to these rules, and one draw needn't show every extreme that they name: `assignment`: in each aligned block of 256 rows (the rows of one device) no cluster is named by more than 16 rows; every cluster is named by some row.
All inputs are finite; a program needn't handle non-finite values.
Results may differ from a plain program's by a relative error of at most 0.0016.
Values may be sent and summed in bfloat16 or wider, within the bound.
No kernel may reach another device: no remote copies, remote signals or barrier semaphores. Data moves between devices by JAX's collectives and lax.ppermute only.
A program may use at most 64 MiB of HBM per device.

v0:
```python
import jax
import jax.numpy as jnp
from jax import lax
from jax.sharding import PartitionSpec as P

CLU_DEV = 2
EPS = 1e-06


def normalize(embeddings):
    values = embeddings.astype(jnp.float32)
    scale = lax.rsqrt(jnp.sum(values * values, axis=-1, keepdims=True) + EPS)
    return (values * scale).astype(jnp.bfloat16)


def slot_index(cluster, groups, most):
    count = cluster.shape[0]
    order = jnp.argsort(cluster, stable=True)
    ranked = cluster[order]
    first = jnp.searchsorted(ranked, ranked, side="left")
    rank_sorted = jnp.arange(count, dtype=jnp.int32) - first
    rank = jnp.zeros((count,), jnp.int32).at[order].set(rank_sorted)
    local = cluster % CLU_DEV
    owner = cluster // CLU_DEV
    return (local * groups + owner) * most + rank


def cluster_scores(pieces):
    rows, flags = pieces
    items = rows.shape[0]
    width = rows.shape[1] * rows.shape[2]
    rows = rows.reshape(items, width, rows.shape[3])
    flags = flags.reshape(items, width)
    offsets = jnp.arange(width, dtype=jnp.int32)
    distinct = offsets[:, None] != offsets[None, :]

    def single(pair):
        block, marks = pair
        gram = lax.dot_general(
            block, block, (((1,), (1,)), ((), ())), preferred_element_type=jnp.float32
        )
        keep = distinct & (marks > 0)[None, :]
        best = jnp.max(jnp.where(keep, gram, jnp.float32(-2.0)), axis=1)
        return jnp.maximum(best, jnp.float32(-1.0))

    best = lax.map(single, (rows, flags))
    return best.reshape(items, 1, width)


def shards(embeddings, assignment):
    groups = lax.axis_size("clu")
    count = embeddings.shape[0]
    width = embeddings.shape[1]
    most = 2 * count // (CLU_DEV * groups)
    unit = normalize(embeddings)
    cluster = assignment[:, 0]
    slot = slot_index(cluster, groups, most)
    total = CLU_DEV * groups * most
    outgoing = jnp.zeros((total, width), jnp.bfloat16).at[slot].set(unit)
    marks = jnp.zeros((total,), jnp.bfloat16).at[slot].set(jnp.ones((count,), jnp.bfloat16))
    outgoing = outgoing.reshape(CLU_DEV, groups, most, width)
    marks = marks.reshape(CLU_DEV, groups, most)
    arrived = (
        lax.all_to_all(outgoing, "clu", split_axis=1, concat_axis=2, tiled=True),
        lax.all_to_all(marks, "clu", split_axis=1, concat_axis=2, tiled=True),
    )
    best = cluster_scores(arrived)
    returned = lax.all_to_all(best, "clu", split_axis=2, concat_axis=1, tiled=True)
    return returned.reshape(total)[slot]


def solution(mesh):
    in_specs = (P(("lang", "clu"), None), P(("lang", "clu"), None))
    out_specs = P(("lang", "clu"))
    return jax.shard_map(shards, mesh=mesh, in_specs=in_specs, out_specs=out_specs, check_vma=False)
```

profile of v0, /device:TPU:0, one launch (start us, length us, event | category | flops | bytes accessed | tf_op | source)
XLA Modules:
  0.0 87.9 jit_solution(13854131566071930487)
XLA Ops:
  0.0 0.0 copy-start
  0.0 0.7 copy-done
  0.7 3.2 %sort.17 = (s32[256]{0:T(256)}, s32[256]{0:T(256)S(1)}) sort(s32[256]{0:T(256)S(1)} %bitcast.15, s32[256]{0:T(256)S(1)} %iota.14), dimensions={0}, to_apply=%region_0.0 | sort | flops 2048 | bytes 4096 | tf_op jit(solution)/shard_map/jit(argsort)/sort | solution.py:18
  3.9 1.9 %gather_fusion.1 = s32[256]{0:T(256)S(1)} fusion(s32[256]{0:T(256)S(1)} %bitcast.16, s32[1024]{0:T(1024)S(1)} %pad_clamp_fusion.2), kind=kCustom, calls=%fused_computation.1 | custom fusion | bytes 3072 | tf_op jit(solution)/shard_map/gather | solution.py:19
  5.8 0.0 copy-start.1
  5.8 18.4 %while.37 = (s32[]{:T(128)}, u32[256]{0:T(256)S(1)}, u32[256]{0:T(256)S(1)}, s32[256]{0:T(256)S(1)}, s32[]{:T(128)}, /*index=5*/s32[]{:T(128)}, s32[]{}) while((s32[]{:T(128)}, u32[256]{0:T(256)S(1)}, u32[256]{0:T(256)S(1)}, s32[256]{0:T(256)S(1)}, s32[]{:T(128)}, /*index=5*/s32[]{:T(128)}, s32[]{}) %tuple.52), condition=%wide.region_2.3_spmd.clone, body=%wide.region_1.0_spmd.clone.sunk | while | flops 5636 | bytes 22117 | solution.py:20
  5.9 1.9 %gather_fusion = s32[256]{0:T(256)S(1)} fusion(s32[256]{0:T(256)S(1)} %get-tuple-element.217, u32[1024]{0:T(1024)S(1)} %pad_clamp_fusion.4), kind=kCustom, calls=%fused_computation.clone.clone.1 | custom fusion | bytes 3072 | tf_op jit(solution)/shard_map/jit(searchsorted)/jit(_searchsorted_scan_impl)/vmap(jit(_searchsorted_scan_impl))/while/body/eval_jaxpr/gather | solution.py:20
  7.9 1.9 %gather_fusion = s32[256]{0:T(256)S(1)} fusion(s32[256]{0:T(256)S(1)} %get-tuple-element.217, u32[1024]{0:T(1024)S(1)} %pad_clamp_fusion.4), kind=kCustom, calls=%fused_computation.clone.clone.1 | custom fusion | bytes 3072 | tf_op jit(solution)/shard_map/jit(searchsorted)/jit(_searchsorted_scan_impl)/vmap(jit(_searchsorted_scan_impl))/while/body/eval_jaxpr/gather | solution.py:20
  9.9 1.9 %gather_fusion = s32[256]{0:T(256)S(1)} fusion(s32[256]{0:T(256)S(1)} %get-tuple-element.217, u32[1024]{0:T(1024)S(1)} %pad_clamp_fusion.4), kind=kCustom, calls=%fused_computation.clone.clone.1 | custom fusion | bytes 3072 | tf_op jit(solution)/shard_map/jit(searchsorted)/jit(_searchsorted_scan_impl)/vmap(jit(_searchsorted_scan_impl))/while/body/eval_jaxpr/gather | solution.py:20
  12.0 1.9 %gather_fusion = s32[256]{0:T(256)S(1)} fusion(s32[256]{0:T(256)S(1)} %get-tuple-element.217, u32[1024]{0:T(1024)S(1)} %pad_clamp_fusion.4), kind=kCustom, calls=%fused_computation.clone.clone.1 | custom fusion | bytes 3072 | tf_op jit(solution)/shard_map/jit(searchsorted)/jit(_searchsorted_scan_impl)/vmap(jit(_searchsorted_scan_impl))/while/body/eval_jaxpr/gather | solution.py:20
  14.0 1.9 %gather_fusion = s32[256]{0:T(256)S(1)} fusion(s32[256]{0:T(256)S(1)} %get-tuple-element.217, u32[1024]{0:T(1024)S(1)} %pad_clamp_fusion.4), kind=kCustom, calls=%fused_computation.clone.clone.1 | custom fusion | bytes 3072 | tf_op jit(solution)/shard_map/jit(searchsorted)/jit(_searchsorted_scan_impl)/vmap(jit(_searchsorted_scan_impl))/while/body/eval_jaxpr/gather | solution.py:20
  16.1 1.9 %gather_fusion = s32[256]{0:T(256)S(1)} fusion(s32[256]{0:T(256)S(1)} %get-tuple-element.217, u32[1024]{0:T(1024)S(1)} %pad_clamp_fusion.4), kind=kCustom, calls=%fused_computation.clone.clone.1 | custom fusion | bytes 3072 | tf_op jit(solution)/shard_map/jit(searchsorted)/jit(_searchsorted_scan_impl)/vmap(jit(_searchsorted_scan_impl))/while/body/eval_jaxpr/gather | solution.py:20
  18.1 1.9 %gather_fusion = s32[256]{0:T(256)S(1)} fusion(s32[256]{0:T(256)S(1)} %get-tuple-element.217, u32[1024]{0:T(1024)S(1)} %pad_clamp_fusion.4), kind=kCustom, calls=%fused_computation.clone.clone.1 | custom fusion | bytes 3072 | tf_op jit(solution)/shard_map/jit(searchsorted)/jit(_searchsorted_scan_impl)/vmap(jit(_searchsorted_scan_impl))/while/body/eval_jaxpr/gather | solution.py:20
  20.1 1.9 %gather_fusion = s32[256]{0:T(256)S(1)} fusion(s32[256]{0:T(256)S(1)} %get-tuple-element.217, u32[1024]{0:T(1024)S(1)} %pad_clamp_fusion.4), kind=kCustom, calls=%fused_computation.clone.clone.1 | custom fusion | bytes 3072 | tf_op jit(solution)/shard_map/jit(searchsorted)/jit(_searchsorted_scan_impl)/vmap(jit(_searchsorted_scan_impl))/while/body/eval_jaxpr/gather | solution.py:20
  22.2 1.9 %gather_fusion = s32[256]{0:T(256)S(1)} fusion(s32[256]{0:T(256)S(1)} %get-tuple-element.217, u32[1024]{0:T(1024)S(1)} %pad_clamp_fusion.4), kind=kCustom, calls=%fused_computation.clone.clone.1 | custom fusion | bytes 3072 | tf_op jit(solution)/shard_map/jit(searchsorted)/jit(_searchsorted_scan_impl)/vmap(jit(_searchsorted_scan_impl))/while/body/eval_jaxpr/gather | solution.py:20
  24.2 1.4 %scatter_custom_fusion = s32[256]{0:T(256)S(1)} fusion(s32[256]{0:T(256)S(1)} %compare_select_fusion.1, s32[256]{0:T(256)S(1)} %convert_subtract_fusion, s32[]{:T(128)} %constant.83.clone.1), kind=kCustom, calls=%fused_computation.42 | custom fusion | bytes 1028 | tf_op jit(solution)/shard_map/scatter | solution.py:22
  25.6 2.2 %scatter_custom_fusion.1 = bf16[512]{0:T(512)(128)(2,1)S(1)} fusion(s32[256]{0:T(256)S(1)} %compare_select_fusion, bf16[256]{0:T(256)(128)(2,1)S(1)} %broadcast.47, bf16[]{:T(256)} %constant.85.clone.1), kind=kCustom, calls=%fused_computation.44 | custom fusion | bytes 1026 | tf_op jit(solution)/shard_map/scatter | solution.py:60
  27.8 0.1 reshape.45
  27.9 0.6 copy.5
  28.5 7.4 %all-to-all-start = ((bf16[2,16,16]{2,0,1:T(2,128)(2,1)}), bf16[2,16,16]{2,0,1:T(2,128)(2,1)S(1)}, u32[]{:S(2)}, u32[]{:S(2)}) async-start(bf16[2,16,16]{2,0,1:T(2,128)(2,1)} %copy.5), calls=%async_computation | async-start | bytes 16384 | tf_op jit(solution)/shard_map/all_to_all | solution.py:65
  35.9 0.0 copy-done.1
  35.9 0.2 fusion.9
  36.1 2.0 %scatter_custom_fusion.2 = bf16[512,1024]{1,0:T(8,128)(2,1)S(1)} fusion(s32[256]{0:T(256)S(1)} %compare_select_fusion, bf16[256,1024]{1,0:T(8,128)(2,1)S(1)} %copy-done.1, f32[256]{0:T(256)S(1)} %add_rsqrt_fusion, bf16[]{:T(256)} %constant.85.clone.1), kind=kCustom, calls=%fused_computation.26 | custom fusion | flops 786432 | bytes 1573890 | tf_op jit(solution)/shard_map/scatter | solution.py:59
  38.1 1.1 %copy.7 = bf16[2,16,16,1024]{3,2,0,1:T(8,128)(2,1)} copy(bf16[2,16,16,1024]{3,2,1,0:T(8,128)(2,1)S(1)} %bitcast.19) | data formatting | bytes 2097152 | tf_op jit(solution)/shard_map/reshape | solution.py:61
  39.2 3.2 %all-to-all-done = bf16[2,16,16]{2,0,1:T(2,128)(2,1)S(1)} async-done(((bf16[2,16,16]{2,0,1:T(2,128)(2,1)}), bf16[2,16,16]{2,0,1:T(2,128)(2,1)S(1)}, u32[]{:S(2)}, u32[]{:S(2)}) %all-to-all-start) | async-done | bytes 1056 | tf_op jit(solution)/shard_map/all_to_all | solution.py:65
  42.3 3.7 %all-to-all-start.1 = ((bf16[2,16,16,1024]{3,2,0,1:T(8,128)(2,1)}), bf16[2,16,16,1024]{3,2,0,1:T(8,128)(2,1)S(1)}, u32[]{:S(2)}, u32[]{:S(2)}) async-start(bf16[2,16,16,1024]{3,2,0,1:T(8,128)(2,1)} %copy.7), calls=%async_computation.1 | async-start | bytes 2097152 | tf_op jit(solution)/shard_map/all_to_all | solution.py:64
  46.0 0.1 reshape.46
  46.1 22.7 %all-to-all-done.1 = bf16[2,16,16,1024]{3,2,0,1:T(8,128)(2,1)S(1)} async-done(((bf16[2,16,16,1024]{3,2,0,1:T(8,128)(2,1)}), bf16[2,16,16,1024]{3,2,0,1:T(8,128)(2,1)S(1)}, u32[]{:S(2)}, u32[]{:S(2)}) %all-to-all-start.1) | async-done | bytes 1048608 | tf_op jit(solution)/shard_map/all_to_all | solution.py:64
  68.8 0.1 copy.8
  68.9 0.9 %while.36 = (s32[]{:T(128)}, f32[2,256]{1,0:T(2,128)S(1)}, bf16[2,256]{1,0:T(2,128)(2,1)S(1)}, bf16[2,256,1024]{2,1,0:T(8,128)(2,1)S(1)}, s32[]{:T(128)}, /*index=5*/s32[]{:T(128)}) while((s32[]{:T(128)}, f32[2,256]{1,0:T(2,128)S(1)}, bf16[2,256]{1,0:T(2,128)(2,1)S(1)}, bf16[2,256,1024]{2,1,0:T(8,128)(2,1)S(1)}, s32[]{:T(128)}, ...), condition=%wide.region_9.10_spmd.clone, body=%wide.region_7.9_spmd.clone.sunk | while | flops 134480640 | bytes 530769 | solution.py:46
  69.0 0.4 fusion.26
  69.4 0.4 fusion.26
  69.8 0.8 copy.9
  70.6 6.7 %all-to-all-start.2 = ((f32[2,1,256]{0,1,2:T(1,128)}), f32[2,1,256]{0,1,2:T(1,128)S(1)}, u32[]{:S(2)}, u32[]{:S(2)}) async-start(f32[2,1,256]{0,1,2:T(1,128)} %bitcast.3), calls=%async_computation.2 | async-start | bytes 262144 | tf_op jit(solution)/shard_map/all_to_all | solution.py:68
  77.4 7.9 %all-to-all-done.2 = f32[2,1,256]{0,1,2:T(1,128)S(1)} async-done(((f32[2,1,256]{0,1,2:T(1,128)}), f32[2,1,256]{0,1,2:T(1,128)S(1)}, u32[]{:S(2)}, u32[]{:S(2)}) %all-to-all-start.2) | async-done | bytes 2080 | tf_op jit(solution)/shard_map/all_to_all | solution.py:68
  85.3 0.1 copy.10
  85.4 2.5 %gather_fusion.2 = f32[256]{0:T(256)} fusion(f32[512]{0:T(512)S(1)} %bitcast.18, s32[1024]{0:T(1024)S(1)} %pad_clamp_fusion.1), kind=kCustom, calls=%fused_computation.2 | custom fusion | bytes 3072 | tf_op jit(solution)/shard_map/gather | solution.py:69
  (64 shorter events, 0.6 us)
Async XLA Ops:
  0.0 0.7 copy-start
  5.8 30.1 %copy-start.1 = (bf16[256,1024]{1,0:T(8,128)(2,1)S(1)}, bf16[256,1024]{1,0:T(8,128)(2,1)}, u32[]{:S(2)}) copy-start(bf16[256,1024]{1,0:T(8,128)(2,1)} %param.6) | copy-start | bytes 1572868
  28.5 13.8 %all-to-all-start = ((bf16[2,16,16]{2,0,1:T(2,128)(2,1)}), bf16[2,16,16]{2,0,1:T(2,128)(2,1)S(1)}, u32[]{:S(2)}, u32[]{:S(2)}) async-start(bf16[2,16,16]{2,0,1:T(2,128)(2,1)} %copy.5), calls=%async_computation | async-start | bytes 16384 | tf_op jit(solution)/shard_map/all_to_all | solution.py:65
  42.3 26.5 %all-to-all-start.1 = ((bf16[2,16,16,1024]{3,2,0,1:T(8,128)(2,1)}), bf16[2,16,16,1024]{3,2,0,1:T(8,128)(2,1)S(1)}, u32[]{:S(2)}, u32[]{:S(2)}) async-start(bf16[2,16,16,1024]{3,2,0,1:T(8,128)(2,1)} %copy.7), calls=%async_computation.1 | async-start | bytes 2097152 | tf_op jit(solution)/shard_map/all_to_all | solution.py:64
  70.6 14.6 %all-to-all-start.2 = ((f32[2,1,256]{0,1,2:T(1,128)}), f32[2,1,256]{0,1,2:T(1,128)S(1)}, u32[]{:S(2)}, u32[]{:S(2)}) async-start(f32[2,1,256]{0,1,2:T(1,128)} %bitcast.3), calls=%async_computation.2 | async-start | bytes 262144 | tf_op jit(solution)/shard_map/all_to_all | solution.py:68
where the time goes:
time: 88.2 us; the launch traced here: 87.9 us
  waiting for transfers between devices  33.8 us (38%)
  local copies, waits for them, and re-layouts  29.1 us (33%)
  starting transfers between devices  17.8 us (20%)
  other arithmetic  5.78 us (7%)
    all_to_all x1, waiting for transfers between devices, shards(): lax.all_to_all(outgoing, 'clu', split_axis=1, concat_axis=2, tiled=True)  22.7 us
    gather x9, local copies, waits for them, and re-layouts, slot_index(): first = jnp.searchsorted(ranked, ranked, side='left')  17.5 us
    all_to_all x1, waiting for transfers between devices, shards(): lax.all_to_all(best, 'clu', split_axis=2, concat_axis=1, tiled=True)  7.89 us
    all_to_all x1, starting transfers between devices, shards(): lax.all_to_all(marks, 'clu', split_axis=1, concat_axis=2, tiled=True)  7.39 us
    all_to_all x1, starting transfers between devices, shards(): lax.all_to_all(best, 'clu', split_axis=2, concat_axis=1, tiled=True)  6.74 us
    all_to_all x1, starting transfers between devices, shards(): lax.all_to_all(outgoing, 'clu', split_axis=1, concat_axis=2, tiled=True)  3.65 us
    all_to_all x1, waiting for transfers between devices, shards(): lax.all_to_all(marks, 'clu', split_axis=1, concat_axis=2, tiled=True)  3.18 us
    sort x1, other arithmetic, slot_index(): order = jnp.argsort(cluster, stable=True)  3.16 us
  transfers between devices with their start and end apart: 3, of which 3 were waited for; matrix products, arithmetic and copies ran while one was open for 4% of the time, Pallas kernels for 0%

commit v1 on v0

--- a/solution.py
+++ b/solution.py
@@ -5,6 +5,29 @@
 
 CLU_DEV = 2
 EPS = 1e-06
+
+
+def get_indices(out_dim, ndim_at, raw):
+    local_part = lax.axis_size("clu")
+    arr_now = lax.axis_index("clu")
+    k_now, w_next = (local_part, arr_now)
+    opened = raw.shape[ndim_at] // k_now
+    work_now = list(raw.shape)
+    work_now[ndim_at] = opened
+    last = work_now[out_dim]
+    work_now[out_dim] = last * k_now
+    long_array = jnp.zeros(work_now, raw.dtype)
+    p = 0
+    while p < k_now:
+        answer = lax.dynamic_slice_in_dim(raw, (w_next ^ p) * opened, opened, axis=ndim_at)
+        if p:
+            aux = tuple(((m, m ^ p) for m in range(k_now)))
+            answer = lax.ppermute(answer, "clu", aux)
+        long_array = lax.dynamic_update_slice_in_dim(
+            long_array, answer, (w_next ^ p) * last, axis=out_dim
+        )
+        p += 1
+    return long_array
 
 
 def normalize(embeddings):
@@ -65,7 +88,7 @@
         lax.all_to_all(marks, "clu", split_axis=1, concat_axis=2, tiled=True),
     )
     best = cluster_scores(arrived)
-    returned = lax.all_to_all(best, "clu", split_axis=2, concat_axis=1, tiled=True)
+    returned = get_indices(1, 2, best)
     return returned.reshape(total)[slot]
 
 

time: 88.2 us -> 101 us (1.15)
  starting transfers between devices: 17.8 us -> 34.3 us
  waiting for transfers between devices: 33.8 us -> 30.2 us
    ppermute x0 -> x15, starting transfers between devices: none -> 23.2 us  [get_indices(): answer = lax.ppermute(answer, 'clu', aux)]
    all_to_all x1 -> x0, waiting for transfers between devices: 7.89 us -> none  [shards(): lax.all_to_all(best, 'clu', split_axis=2, concat_axis=1, tiled=True)]
    all_to_all x1 -> x0, starting transfers between devices: 6.74 us -> none  [shards(): lax.all_to_all(best, 'clu', split_axis=2, concat_axis=1, tiled=True)]
    ppermute x0 -> x15, waiting for transfers between devices: none -> 4.57 us  [get_indices(): answer = lax.ppermute(answer, 'clu', aux)]
  transfers between devices with their start and end apart: 3 -> 17, of which waited for: 3 -> 4; matrix products, arithmetic and copies ran while one was open for 4% -> 4% of each run, Pallas kernels for 0% -> 0%
where the time goes in v1:
time: 101 us
  starting transfers between devices  34.3 us (34%)
  waiting for transfers between devices  30.2 us (30%)
  local copies, waits for them, and re-layouts  28.9 us (29%)
  other arithmetic  5.78 us (6%)
    ppermute x15, starting transfers between devices, get_indices(): answer = lax.ppermute(answer, 'clu', aux)  23.2 us
    all_to_all x1, waiting for transfers between devices, shards(): lax.all_to_all(outgoing, 'clu', split_axis=1, concat_axis=2, tiled=True)  22.4 us
    gather x9, local copies, waits for them, and re-layouts, slot_index(): first = jnp.searchsorted(ranked, ranked, side='left')  17.5 us
    all_to_all x1, starting transfers between devices, shards(): lax.all_to_all(marks, 'clu', split_axis=1, concat_axis=2, tiled=True)  7.39 us
    ppermute x15, waiting for transfers between devices, get_indices(): answer = lax.ppermute(answer, 'clu', aux)  4.57 us
    all_to_all x1, starting transfers between devices, shards(): lax.all_to_all(outgoing, 'clu', split_axis=1, concat_axis=2, tiled=True)  3.65 us
    all_to_all x1, waiting for transfers between devices, shards(): lax.all_to_all(marks, 'clu', split_axis=1, concat_axis=2, tiled=True)  3.2 us
    sort x1, other arithmetic, slot_index(): order = jnp.argsort(cluster, stable=True)  3.16 us
  transfers between devices with their start and end apart: 17, of which 4 were waited for; matrix products, arithmetic and copies ran while one was open for 4% of the time, Pallas kernels for 0%

profile of v1, /device:TPU:0, one launch (start us, length us, event | category | flops | bytes accessed | tf_op | source)
XLA Modules:
  0.0 100.9 jit_solution(7162420280068988856)
XLA Ops:
  0.0 0.7 copy-done
  0.7 3.2 %sort.17 = (s32[256]{0:T(256)}, s32[256]{0:T(256)S(1)}) sort(s32[256]{0:T(256)S(1)} %bitcast.59, s32[256]{0:T(256)S(1)} %iota.14), dimensions={0}, to_apply=%region_0.0 | sort | flops 2048 | bytes 4096 | tf_op jit(solution)/shard_map/jit(argsort)/sort | solution.py:41
  3.9 1.9 %gather_fusion.1 = s32[256]{0:T(256)S(1)} fusion(s32[256]{0:T(256)S(1)} %bitcast.60, s32[1024]{0:T(1024)S(1)} %pad_clamp_fusion.2), kind=kCustom, calls=%fused_computation.1 | custom fusion | bytes 3072 | tf_op jit(solution)/shard_map/gather | solution.py:42
  5.8 0.0 copy-start.1
  5.8 18.4 %while.37 = (s32[]{:T(128)}, u32[256]{0:T(256)S(1)}, u32[256]{0:T(256)S(1)}, s32[256]{0:T(256)S(1)}, s32[]{:T(128)}, /*index=5*/s32[]{:T(128)}, s32[]{}) while((s32[]{:T(128)}, u32[256]{0:T(256)S(1)}, u32[256]{0:T(256)S(1)}, s32[256]{0:T(256)S(1)}, s32[]{:T(128)}, /*index=5*/s32[]{:T(128)}, s32[]{}) %tuple.67), condition=%wide.region_2.3_spmd.clone, body=%wide.region_1.0_spmd.clone.sunk | while | flops 5636 | bytes 22117 | solution.py:43
  5.9 1.9 %gather_fusion = s32[256]{0:T(256)S(1)} fusion(s32[256]{0:T(256)S(1)} %get-tuple-element.233, u32[1024]{0:T(1024)S(1)} %pad_clamp_fusion.4), kind=kCustom, calls=%fused_computation.clone.clone.1 | custom fusion | bytes 3072 | tf_op jit(solution)/shard_map/jit(searchsorted)/jit(_searchsorted_scan_impl)/vmap(jit(_searchsorted_scan_impl))/while/body/eval_jaxpr/gather | solution.py:43
  7.9 1.9 %gather_fusion = s32[256]{0:T(256)S(1)} fusion(s32[256]{0:T(256)S(1)} %get-tuple-element.233, u32[1024]{0:T(1024)S(1)} %pad_clamp_fusion.4), kind=kCustom, calls=%fused_computation.clone.clone.1 | custom fusion | bytes 3072 | tf_op jit(solution)/shard_map/jit(searchsorted)/jit(_searchsorted_scan_impl)/vmap(jit(_searchsorted_scan_impl))/while/body/eval_jaxpr/gather | solution.py:43
  9.9 1.9 %gather_fusion = s32[256]{0:T(256)S(1)} fusion(s32[256]{0:T(256)S(1)} %get-tuple-element.233, u32[1024]{0:T(1024)S(1)} %pad_clamp_fusion.4), kind=kCustom, calls=%fused_computation.clone.clone.1 | custom fusion | bytes 3072 | tf_op jit(solution)/shard_map/jit(searchsorted)/jit(_searchsorted_scan_impl)/vmap(jit(_searchsorted_scan_impl))/while/body/eval_jaxpr/gather | solution.py:43
  12.0 1.9 %gather_fusion = s32[256]{0:T(256)S(1)} fusion(s32[256]{0:T(256)S(1)} %get-tuple-element.233, u32[1024]{0:T(1024)S(1)} %pad_clamp_fusion.4), kind=kCustom, calls=%fused_computation.clone.clone.1 | custom fusion | bytes 3072 | tf_op jit(solution)/shard_map/jit(searchsorted)/jit(_searchsorted_scan_impl)/vmap(jit(_searchsorted_scan_impl))/while/body/eval_jaxpr/gather | solution.py:43
  14.0 1.9 %gather_fusion = s32[256]{0:T(256)S(1)} fusion(s32[256]{0:T(256)S(1)} %get-tuple-element.233, u32[1024]{0:T(1024)S(1)} %pad_clamp_fusion.4), kind=kCustom, calls=%fused_computation.clone.clone.1 | custom fusion | bytes 3072 | tf_op jit(solution)/shard_map/jit(searchsorted)/jit(_searchsorted_scan_impl)/vmap(jit(_searchsorted_scan_impl))/while/body/eval_jaxpr/gather | solution.py:43
  16.1 1.9 %gather_fusion = s32[256]{0:T(256)S(1)} fusion(s32[256]{0:T(256)S(1)} %get-tuple-element.233, u32[1024]{0:T(1024)S(1)} %pad_clamp_fusion.4), kind=kCustom, calls=%fused_computation.clone.clone.1 | custom fusion | bytes 3072 | tf_op jit(solution)/shard_map/jit(searchsorted)/jit(_searchsorted_scan_impl)/vmap(jit(_searchsorted_scan_impl))/while/body/eval_jaxpr/gather | solution.py:43
  18.1 1.9 %gather_fusion = s32[256]{0:T(256)S(1)} fusion(s32[256]{0:T(256)S(1)} %get-tuple-element.233, u32[1024]{0:T(1024)S(1)} %pad_clamp_fusion.4), kind=kCustom, calls=%fused_computation.clone.clone.1 | custom fusion | bytes 3072 | tf_op jit(solution)/shard_map/jit(searchsorted)/jit(_searchsorted_scan_impl)/vmap(jit(_searchsorted_scan_impl))/while/body/eval_jaxpr/gather | solution.py:43
  20.1 1.9 %gather_fusion = s32[256]{0:T(256)S(1)} fusion(s32[256]{0:T(256)S(1)} %get-tuple-element.233, u32[1024]{0:T(1024)S(1)} %pad_clamp_fusion.4), kind=kCustom, calls=%fused_computation.clone.clone.1 | custom fusion | bytes 3072 | tf_op jit(solution)/shard_map/jit(searchsorted)/jit(_searchsorted_scan_impl)/vmap(jit(_searchsorted_scan_impl))/while/body/eval_jaxpr/gather | solution.py:43
  22.2 1.9 %gather_fusion = s32[256]{0:T(256)S(1)} fusion(s32[256]{0:T(256)S(1)} %get-tuple-element.233, u32[1024]{0:T(1024)S(1)} %pad_clamp_fusion.4), kind=kCustom, calls=%fused_computation.clone.clone.1 | custom fusion | bytes 3072 | tf_op jit(solution)/shard_map/jit(searchsorted)/jit(_searchsorted_scan_impl)/vmap(jit(_searchsorted_scan_impl))/while/body/eval_jaxpr/gather | solution.py:43
  24.2 1.4 %scatter_custom_fusion = s32[256]{0:T(256)S(1)} fusion(s32[256]{0:T(256)S(1)} %compare_select_fusion.1, s32[256]{0:T(256)S(1)} %convert_subtract_fusion, s32[]{:T(128)} %constant.104.clone.1), kind=kCustom, calls=%fused_computation.73 | custom fusion | bytes 1028 | tf_op jit(solution)/shard_map/scatter | solution.py:45
  25.6 2.2 %scatter_custom_fusion.1 = bf16[512]{0:T(512)(128)(2,1)S(1)} fusion(s32[256]{0:T(256)S(1)} %compare_select_fusion, bf16[256]{0:T(256)(128)(2,1)S(1)} %broadcast.50, bf16[]{:T(256)} %constant.105.clone.1), kind=kCustom, calls=%fused_computation.75 | custom fusion | bytes 1026 | tf_op jit(solution)/shard_map/scatter | solution.py:83
  27.8 0.1 reshape.55
  27.9 0.6 copy.36
  28.5 7.4 %all-to-all-start = ((bf16[2,16,16]{2,0,1:T(2,128)(2,1)}), bf16[2,16,16]{2,0,1:T(2,128)(2,1)S(1)}, u32[]{:S(2)}, u32[]{:S(2)}) async-start(bf16[2,16,16]{2,0,1:T(2,128)(2,1)} %copy.36), calls=%async_computation | async-start | bytes 16384 | tf_op jit(solution)/shard_map/all_to_all | solution.py:88
  35.9 0.0 copy-done.1
  35.9 0.2 fusion.9
  36.1 2.0 %scatter_custom_fusion.2 = bf16[512,1024]{1,0:T(8,128)(2,1)S(1)} fusion(s32[256]{0:T(256)S(1)} %compare_select_fusion, bf16[256,1024]{1,0:T(8,128)(2,1)S(1)} %copy-done.1, f32[256]{0:T(256)S(1)} %add_rsqrt_fusion, bf16[]{:T(256)} %constant.105.clone.1), kind=kCustom, calls=%fused_computation.26 | custom fusion | flops 786432 | bytes 1573890 | tf_op jit(solution)/shard_map/scatter | solution.py:82
  38.1 1.0 %copy.38 = bf16[2,16,16,1024]{3,2,0,1:T(8,128)(2,1)} copy(bf16[2,16,16,1024]{3,2,1,0:T(8,128)(2,1)S(1)} %bitcast.62) | data formatting | bytes 2097152 | tf_op jit(solution)/shard_map/reshape | solution.py:84
  39.1 3.2 %all-to-all-done = bf16[2,16,16]{2,0,1:T(2,128)(2,1)S(1)} async-done(((bf16[2,16,16]{2,0,1:T(2,128)(2,1)}), bf16[2,16,16]{2,0,1:T(2,128)(2,1)S(1)}, u32[]{:S(2)}, u32[]{:S(2)}) %all-to-all-start) | async-done | bytes 1056 | tf_op jit(solution)/shard_map/all_to_all | solution.py:88
  42.3 3.7 %all-to-all-start.1 = ((bf16[2,16,16,1024]{3,2,0,1:T(8,128)(2,1)}), bf16[2,16,16,1024]{3,2,0,1:T(8,128)(2,1)S(1)}, u32[]{:S(2)}, u32[]{:S(2)}) async-start(bf16[2,16,16,1024]{3,2,0,1:T(8,128)(2,1)} %copy.38), calls=%async_computation.1 | async-start | bytes 2097152 | tf_op jit(solution)/shard_map/all_to_all | solution.py:87
  46.3 0.1 reshape.56
  46.4 22.4 %all-to-all-done.1 = bf16[2,16,16,1024]{3,2,0,1:T(8,128)(2,1)S(1)} async-done(((bf16[2,16,16,1024]{3,2,0,1:T(8,128)(2,1)}), bf16[2,16,16,1024]{3,2,0,1:T(8,128)(2,1)S(1)}, u32[]{:S(2)}, u32[]{:S(2)}) %all-to-all-start.1) | async-done | bytes 1048608 | tf_op jit(solution)/shard_map/all_to_all | solution.py:87
  68.8 0.1 copy.39
  69.0 0.9 while.36
  69.0 0.4 fusion.41
  69.4 0.4 fusion.41
  69.8 0.1 fusion.31
  70.0 0.7 collective-permute-start
  70.7 2.0 %collective-permute-start.1 = (f32[2,1,16]{2,0,1:T(2,128)S(1)}, f32[2,1,16]{2,0,1:T(2,128)S(1)}, u32[]{:S(2)}, u32[]{:S(2)}) collective-permute-start(f32[2,1,16]{2,0,1:T(2,128)S(1)} %get-tuple-element.159), channel_id=1, source_target_pairs={{0,2},{1,3},{2,0},{3,1},{4,6},{5,7},{6,4},{7,5},{8,10},{9,11},{10,... | collective-permute-start | bytes 392 | tf_op jit(solution)/shard_map/ppermute | solution.py:25
  72.7 0.0 collective-permute-start.2
  72.7 2.8 %collective-permute-start.3 = (f32[2,1,16]{2,0,1:T(2,128)S(1)}, f32[2,1,16]{2,0,1:T(2,128)S(1)}, u32[]{:S(2)}, u32[]{:S(2)}) collective-permute-start(f32[2,1,16]{2,0,1:T(2,128)S(1)} %get-tuple-element.157), channel_id=1, source_target_pairs={{0,4},{1,5},{2,6},{3,7},{4,0},{5,1},{6,2},{7,3},{8,12},{9,13},{10,... | collective-permute-start | bytes 392 | tf_op jit(solution)/shard_map/ppermute | solution.py:25
  75.5 0.3 collective-permute-start.4
  75.9 0.0 collective-permute-done
  75.9 2.6 %collective-permute-start.5 = (f32[2,1,16]{2,0,1:T(2,128)S(1)}, f32[2,1,16]{2,0,1:T(2,128)S(1)}, u32[]{:S(2)}, u32[]{:S(2)}) collective-permute-start(f32[2,1,16]{2,0,1:T(2,128)S(1)} %get-tuple-element.155), channel_id=1, source_target_pairs={{0,6},{1,7},{2,4},{3,5},{4,2},{5,3},{6,0},{7,1},{8,14},{9,15},{10,... | collective-permute-start | bytes 392 | tf_op jit(solution)/shard_map/ppermute | solution.py:25
  78.5 0.0 collective-permute-done.1
  78.5 0.1 collective-permute-start.6
  78.7 0.0 collective-permute-done.2
  78.7 2.9 %collective-permute-start.7 = (f32[2,1,16]{2,0,1:T(2,128)S(1)}, f32[2,1,16]{2,0,1:T(2,128)S(1)}, u32[]{:S(2)}, u32[]{:S(2)}) collective-permute-start(f32[2,1,16]{2,0,1:T(2,128)S(1)} %get-tuple-element.153), channel_id=1, source_target_pairs={{0,8},{1,9},{2,10},{3,11},{4,12},{5,13},{6,14},{7,15},{8,0},{9,1},... | collective-permute-start | bytes 392 | tf_op jit(solution)/shard_map/ppermute | solution.py:25
  81.6 0.0 collective-permute-done.3
  81.6 0.1 collective-permute-start.8
  81.7 0.0 collective-permute-done.4
  81.8 2.2 %collective-permute-start.9 = (f32[2,1,16]{2,0,1:T(2,128)S(1)}, f32[2,1,16]{2,0,1:T(2,128)S(1)}, u32[]{:S(2)}, u32[]{:S(2)}) collective-permute-start(f32[2,1,16]{2,0,1:T(2,128)S(1)} %get-tuple-element.151), channel_id=1, source_target_pairs={{0,10},{1,11},{2,8},{3,9},{4,14},{5,15},{6,12},{7,13},{8,2},{9,3},... | collective-permute-start | bytes 392 | tf_op jit(solution)/shard_map/ppermute | solution.py:25
  83.9 0.0 collective-permute-done.5
  83.9 1.3 %collective-permute-start.10 = (f32[2,1,16]{2,0,1:T(2,128)S(1)}, f32[2,1,16]{2,0,1:T(2,128)S(1)}, u32[]{:S(2)}, u32[]{:S(2)}) collective-permute-start(f32[2,1,16]{2,0,1:T(2,128)S(1)} %get-tuple-element.150), channel_id=1, source_target_pairs={{0,11},{1,10},{2,9},{3,8},{4,15},{5,14},{6,13},{7,12},{8,3},{9,2},... | collective-permute-start | bytes 392 | tf_op jit(solution)/shard_map/ppermute | solution.py:25
  85.2 0.0 collective-permute-done.6
  85.2 2.4 %collective-permute-start.11 = (f32[2,1,16]{2,0,1:T(2,128)S(1)}, f32[2,1,16]{2,0,1:T(2,128)S(1)}, u32[]{:S(2)}, u32[]{:S(2)}) collective-permute-start(f32[2,1,16]{2,0,1:T(2,128)S(1)} %get-tuple-element.149), channel_id=1, source_target_pairs={{0,12},{1,13},{2,14},{3,15},{4,8},{5,9},{6,10},{7,11},{8,4},{9,5},... | collective-permute-start | bytes 392 | tf_op jit(solution)/shard_map/ppermute | solution.py:25
  87.6 0.0 collective-permute-done.7
  87.6 1.6 %collective-permute-start.12 = (f32[2,1,16]{2,0,1:T(2,128)S(1)}, f32[2,1,16]{2,0,1:T(2,128)S(1)}, u32[]{:S(2)}, u32[]{:S(2)}) collective-permute-start(f32[2,1,16]{2,0,1:T(2,128)S(1)} %get-tuple-element.148), channel_id=1, source_target_pairs={{0,13},{1,12},{2,15},{3,14},{4,9},{5,8},{6,11},{7,10},{8,5},{9,4},... | collective-permute-start | bytes 392 | tf_op jit(solution)/shard_map/ppermute | solution.py:25
  89.2 0.0 collective-permute-done.8
  89.2 3.3 %collective-permute-start.13 = (f32[2,1,16]{2,0,1:T(2,128)S(1)}, f32[2,1,16]{2,0,1:T(2,128)S(1)}, u32[]{:S(2)}, u32[]{:S(2)}) collective-permute-start(f32[2,1,16]{2,0,1:T(2,128)S(1)} %get-tuple-element.147), channel_id=1, source_target_pairs={{0,14},{1,15},{2,12},{3,13},{4,10},{5,11},{6,8},{7,9},{8,6},{9,7},... | collective-permute-start | bytes 392 | tf_op jit(solution)/shard_map/ppermute | solution.py:25
  92.5 0.0 collective-permute-done.9
  92.5 1.0 %collective-permute-start.14 = (f32[2,1,16]{2,0,1:T(2,128)S(1)}, f32[2,1,16]{2,0,1:T(2,128)S(1)}, u32[]{:S(2)}, u32[]{:S(2)}) collective-permute-start(f32[2,1,16]{2,0,1:T(2,128)S(1)} %get-tuple-element.146), channel_id=1, source_target_pairs={{0,15},{1,14},{2,13},{3,12},{4,11},{5,10},{6,9},{7,8},{8,7},{9,6},... | collective-permute-start | bytes 392 | tf_op jit(solution)/shard_map/ppermute | solution.py:25
  93.6 0.0 collective-permute-done.10
  93.6 0.0 collective-permute-done.11
  93.6 0.0 collective-permute-done.12
  93.7 1.8 %collective-permute-done.13 = f32[2,1,16]{2,0,1:T(2,128)S(1)} collective-permute-done((f32[2,1,16]{2,0,1:T(2,128)S(1)}, f32[2,1,16]{2,0,1:T(2,128)S(1)}, u32[]{:S(2)}, u32[]{:S(2)}) %collective-permute-start.13) | collective-permute-done | bytes 160 | tf_op jit(solution)/shard_map/ppermute | solution.py:25
  95.6 2.7 %collective-permute-done.14 = f32[2,1,16]{2,0,1:T(2,128)S(1)} collective-permute-done((f32[2,1,16]{2,0,1:T(2,128)S(1)}, f32[2,1,16]{2,0,1:T(2,128)S(1)}, u32[]{:S(2)}, u32[]{:S(2)}) %collective-permute-start.14) | collective-permute-done | bytes 160 | tf_op jit(solution)/shard_map/ppermute | solution.py:25
  98.3 0.1 reshape.59
  98.4 2.5 %gather_fusion.2 = f32[256]{0:T(256)} fusion(f32[512]{0:T(512)S(1)} %reshape.59, s32[1024]{0:T(1024)S(1)} %pad_clamp_fusion.1), kind=kCustom, calls=%fused_computation.2 | custom fusion | bytes 3072 | tf_op jit(solution)/shard_map/gather | solution.py:92
  (81 shorter events, 1.0 us)
Async XLA Ops:
  0.0 0.7 copy-start
  5.8 30.1 %copy-start.1 = (bf16[256,1024]{1,0:T(8,128)(2,1)S(1)}, bf16[256,1024]{1,0:T(8,128)(2,1)}, u32[]{:S(2)}) copy-start(bf16[256,1024]{1,0:T(8,128)(2,1)} %param.6) | copy-start | bytes 1572868
  28.5 13.8 %all-to-all-start = ((bf16[2,16,16]{2,0,1:T(2,128)(2,1)}), bf16[2,16,16]{2,0,1:T(2,128)(2,1)S(1)}, u32[]{:S(2)}, u32[]{:S(2)}) async-start(bf16[2,16,16]{2,0,1:T(2,128)(2,1)} %copy.36), calls=%async_computation | async-start | bytes 16384 | tf_op jit(solution)/shard_map/all_to_all | solution.py:88
  42.3 26.5 %all-to-all-start.1 = ((bf16[2,16,16,1024]{3,2,0,1:T(8,128)(2,1)}), bf16[2,16,16,1024]{3,2,0,1:T(8,128)(2,1)S(1)}, u32[]{:S(2)}, u32[]{:S(2)}) async-start(bf16[2,16,16,1024]{3,2,0,1:T(8,128)(2,1)} %copy.38), calls=%async_computation.1 | async-start | bytes 2097152 | tf_op jit(solution)/shard_map/all_to_all | solution.py:87
  70.0 5.9 %collective-permute-start = (f32[2,1,16]{2,0,1:T(2,128)S(1)}, f32[2,1,16]{2,0,1:T(2,128)S(1)}, u32[]{:S(2)}, u32[]{:S(2)}) collective-permute-start(f32[2,1,16]{2,0,1:T(2,128)S(1)} %get-tuple-element.160), channel_id=1, source_target_pairs={{0,1},{1,0},{2,3},{3,2},{4,5},{5,4},{6,7},{7,6},{8,9},{9,8},{10,11... | collective-permute-start | bytes 392 | tf_op jit(solution)/shard_map/ppermute | solution.py:25
  70.7 7.8 %collective-permute-start.1 = (f32[2,1,16]{2,0,1:T(2,128)S(1)}, f32[2,1,16]{2,0,1:T(2,128)S(1)}, u32[]{:S(2)}, u32[]{:S(2)}) collective-permute-start(f32[2,1,16]{2,0,1:T(2,128)S(1)} %get-tuple-element.159), channel_id=1, source_target_pairs={{0,2},{1,3},{2,0},{3,1},{4,6},{5,7},{6,4},{7,5},{8,10},{9,11},{10,... | collective-permute-start | bytes 392 | tf_op jit(solution)/shard_map/ppermute | solution.py:25
  72.7 6.0 %collective-permute-start.2 = (f32[2,1,16]{2,0,1:T(2,128)S(1)}, f32[2,1,16]{2,0,1:T(2,128)S(1)}, u32[]{:S(2)}, u32[]{:S(2)}) collective-permute-start(f32[2,1,16]{2,0,1:T(2,128)S(1)} %get-tuple-element.158), channel_id=1, source_target_pairs={{0,3},{1,2},{2,1},{3,0},{4,7},{5,6},{6,5},{7,4},{8,11},{9,10},{10,... | collective-permute-start | bytes 392 | tf_op jit(solution)/shard_map/ppermute | solution.py:25
  72.7 8.9 %collective-permute-start.3 = (f32[2,1,16]{2,0,1:T(2,128)S(1)}, f32[2,1,16]{2,0,1:T(2,128)S(1)}, u32[]{:S(2)}, u32[]{:S(2)}) collective-permute-start(f32[2,1,16]{2,0,1:T(2,128)S(1)} %get-tuple-element.157), channel_id=1, source_target_pairs={{0,4},{1,5},{2,6},{3,7},{4,0},{5,1},{6,2},{7,3},{8,12},{9,13},{10,... | collective-permute-start | bytes 392 | tf_op jit(solution)/shard_map/ppermute | solution.py:25
  75.5 6.2 %collective-permute-start.4 = (f32[2,1,16]{2,0,1:T(2,128)S(1)}, f32[2,1,16]{2,0,1:T(2,128)S(1)}, u32[]{:S(2)}, u32[]{:S(2)}) collective-permute-start(f32[2,1,16]{2,0,1:T(2,128)S(1)} %get-tuple-element.156), channel_id=1, source_target_pairs={{0,5},{1,4},{2,7},{3,6},{4,1},{5,0},{6,3},{7,2},{8,13},{9,12},{10,... | collective-permute-start | bytes 392 | tf_op jit(solution)/shard_map/ppermute | solution.py:25
  75.9 8.1 %collective-permute-start.5 = (f32[2,1,16]{2,0,1:T(2,128)S(1)}, f32[2,1,16]{2,0,1:T(2,128)S(1)}, u32[]{:S(2)}, u32[]{:S(2)}) collective-permute-start(f32[2,1,16]{2,0,1:T(2,128)S(1)} %get-tuple-element.155), channel_id=1, source_target_pairs={{0,6},{1,7},{2,4},{3,5},{4,2},{5,3},{6,0},{7,1},{8,14},{9,15},{10,... | collective-permute-start | bytes 392 | tf_op jit(solution)/shard_map/ppermute | solution.py:25
  78.5 6.7 %collective-permute-start.6 = (f32[2,1,16]{2,0,1:T(2,128)S(1)}, f32[2,1,16]{2,0,1:T(2,128)S(1)}, u32[]{:S(2)}, u32[]{:S(2)}) collective-permute-start(f32[2,1,16]{2,0,1:T(2,128)S(1)} %get-tuple-element.154), channel_id=1, source_target_pairs={{0,7},{1,6},{2,5},{3,4},{4,3},{5,2},{6,1},{7,0},{8,15},{9,14},{10,... | collective-permute-start | bytes 392 | tf_op jit(solution)/shard_map/ppermute | solution.py:25
  78.7 9.0 %collective-permute-start.7 = (f32[2,1,16]{2,0,1:T(2,128)S(1)}, f32[2,1,16]{2,0,1:T(2,128)S(1)}, u32[]{:S(2)}, u32[]{:S(2)}) collective-permute-start(f32[2,1,16]{2,0,1:T(2,128)S(1)} %get-tuple-element.153), channel_id=1, source_target_pairs={{0,8},{1,9},{2,10},{3,11},{4,12},{5,13},{6,14},{7,15},{8,0},{9,1},... | collective-permute-start | bytes 392 | tf_op jit(solution)/shard_map/ppermute | solution.py:25
  81.6 7.6 %collective-permute-start.8 = (f32[2,1,16]{2,0,1:T(2,128)S(1)}, f32[2,1,16]{2,0,1:T(2,128)S(1)}, u32[]{:S(2)}, u32[]{:S(2)}) collective-permute-start(f32[2,1,16]{2,0,1:T(2,128)S(1)} %get-tuple-element.152), channel_id=1, source_target_pairs={{0,9},{1,8},{2,11},{3,10},{4,13},{5,12},{6,15},{7,14},{8,1},{9,0},... | collective-permute-start | bytes 392 | tf_op jit(solution)/shard_map/ppermute | solution.py:25
  81.8 10.7 %collective-permute-start.9 = (f32[2,1,16]{2,0,1:T(2,128)S(1)}, f32[2,1,16]{2,0,1:T(2,128)S(1)}, u32[]{:S(2)}, u32[]{:S(2)}) collective-permute-start(f32[2,1,16]{2,0,1:T(2,128)S(1)} %get-tuple-element.151), channel_id=1, source_target_pairs={{0,10},{1,11},{2,8},{3,9},{4,14},{5,15},{6,12},{7,13},{8,2},{9,3},... | collective-permute-start | bytes 392 | tf_op jit(solution)/shard_map/ppermute | solution.py:25
  83.9 9.6 %collective-permute-start.10 = (f32[2,1,16]{2,0,1:T(2,128)S(1)}, f32[2,1,16]{2,0,1:T(2,128)S(1)}, u32[]{:S(2)}, u32[]{:S(2)}) collective-permute-start(f32[2,1,16]{2,0,1:T(2,128)S(1)} %get-tuple-element.150), channel_id=1, source_target_pairs={{0,11},{1,10},{2,9},{3,8},{4,15},{5,14},{6,13},{7,12},{8,3},{9,2},... | collective-permute-start | bytes 392 | tf_op jit(solution)/shard_map/ppermute | solution.py:25
  85.2 8.4 %collective-permute-start.11 = (f32[2,1,16]{2,0,1:T(2,128)S(1)}, f32[2,1,16]{2,0,1:T(2,128)S(1)}, u32[]{:S(2)}, u32[]{:S(2)}) collective-permute-start(f32[2,1,16]{2,0,1:T(2,128)S(1)} %get-tuple-element.149), channel_id=1, source_target_pairs={{0,12},{1,13},{2,14},{3,15},{4,8},{5,9},{6,10},{7,11},{8,4},{9,5},... | collective-permute-start | bytes 392 | tf_op jit(solution)/shard_map/ppermute | solution.py:25
  87.6 6.0 %collective-permute-start.12 = (f32[2,1,16]{2,0,1:T(2,128)S(1)}, f32[2,1,16]{2,0,1:T(2,128)S(1)}, u32[]{:S(2)}, u32[]{:S(2)}) collective-permute-start(f32[2,1,16]{2,0,1:T(2,128)S(1)} %get-tuple-element.148), channel_id=1, source_target_pairs={{0,13},{1,12},{2,15},{3,14},{4,9},{5,8},{6,11},{7,10},{8,5},{9,4},... | collective-permute-start | bytes 392 | tf_op jit(solution)/shard_map/ppermute | solution.py:25
  89.2 6.3 %collective-permute-start.13 = (f32[2,1,16]{2,0,1:T(2,128)S(1)}, f32[2,1,16]{2,0,1:T(2,128)S(1)}, u32[]{:S(2)}, u32[]{:S(2)}) collective-permute-start(f32[2,1,16]{2,0,1:T(2,128)S(1)} %get-tuple-element.147), channel_id=1, source_target_pairs={{0,14},{1,15},{2,12},{3,13},{4,10},{5,11},{6,8},{7,9},{8,6},{9,7},... | collective-permute-start | bytes 392 | tf_op jit(solution)/shard_map/ppermute | solution.py:25
  92.5 5.8 %collective-permute-start.14 = (f32[2,1,16]{2,0,1:T(2,128)S(1)}, f32[2,1,16]{2,0,1:T(2,128)S(1)}, u32[]{:S(2)}, u32[]{:S(2)}) collective-permute-start(f32[2,1,16]{2,0,1:T(2,128)S(1)} %get-tuple-element.146), channel_id=1, source_target_pairs={{0,15},{1,14},{2,13},{3,12},{4,11},{5,10},{6,9},{7,8},{8,7},{9,6},... | collective-permute-start | bytes 392 | tf_op jit(solution)/shard_map/ppermute | solution.py:25
